TPU v7x, 32 devices: a whole 2x2x4 slice. The times are simulated.
32 devices in a mesh: seq: 16 (over z, x, core), chan: 2 (over y).
Axes of the slice: x: 2, y: 2, z: 4, core: 2. Of those that a mesh axis runs over, the one named last changes fastest.
Arguments:
- gate_input: bfloat16 [1024, 4096], P('seq', 'chan'), may hold values from -6 to 6
- key_input: bfloat16 [1024, 4096], P('seq', 'chan'), may hold values from -6 to 6
- value_input: bfloat16 [1024, 4096], P('seq', 'chan'), may hold values from -6 to 6
- decay_rate: float32 [16, 4096], P(None, 'chan'), may hold values from 0.0009765625 to 0.1
- residue: float32 [16, 4096], P(None, 'chan'), may hold values from -1.5 to 1.5
- skip_gain: float32 [4096], P('chan'), may hold values from -3 to 3
- out_weight: bfloat16 [4096, 4096], P('chan', 'seq'), may hold values from -0.125 to 0.125
Outputs:
- mixed: bfloat16 [1024, 4096], P('seq', 'chan')
All inputs are finite; a program needn't handle non-finite values.
Results may differ from a plain program's by a relative error of at most 0.014.
Values may be sent and summed in bfloat16 or wider, within the bound.
A program may use at most 64 MiB of HBM per device.

v0:
```python
import functools

import jax
import jax.numpy as jnp
from jax import lax
from jax.experimental import pallas as pl
from jax.experimental.pallas import tpu as pltpu
from jax.sharding import PartitionSpec as P

MESH = pl.DeviceIdType.MESH
F32 = jnp.float32
BF16 = jnp.bfloat16
LANES = 128
SUB = 8


def one_minus_exp(y):
    series = jnp.ones_like(y)
    for order in range(10, 1, -1):
        series = 1.0 - y * (1.0 / order) * series
    return jnp.where(y < 0.4, y * series, 1.0 - jnp.exp(-y))


def kernel(
    n, n_chan,
    q_hbm, k_hbm, v_hbm, rate_hbm, residue_hbm, skip_ref, w_hbm, out_ref,
    q_ref, k_ref, v_ref, rate_ref, amp_ref, w_ref, w_other, load_sem, w_send, w_recv,
    sig, local, padded, fades, ends, ends_all, starts_all, starts, gathered, partial, landed,
    end_send, end_recv, start_send, start_recv, gather_send, gather_recv, part_send, part_recv,
):
    loads = [
        pltpu.make_async_copy(source, target, load_sem.at[i])
        for i, (source, target) in enumerate([
            (k_hbm, k_ref), (v_hbm, v_ref), (rate_hbm, rate_ref),
            (residue_hbm, amp_ref), (q_hbm, q_ref), (w_hbm, w_ref),
        ])
    ]
    for load in loads:
        load.start()
    tok, chans = q_ref.shape
    modes = rate_ref.shape[0]
    blocks = chans // LANES
    rows = modes * blocks // n
    per_block = modes // rows
    width = w_ref.shape[1]
    per_chan = n // n_chan
    line = n // 4
    tiles = tok // SUB

    me = lax.axis_index("seq")
    chan = lax.axis_index("chan")
    z = me // 4
    x = (me // 2) % 2
    c = me % 2
    barrier = pltpu.get_barrier_semaphore()
    for hop in range(1, n):
        pl.semaphore_signal(
            barrier, inc=1, device_id=(lax.rem(me + hop, n), chan), device_id_type=MESH
        )
    for turn in range(1, n_chan):
        for slot in range(2 * line):
            peer = (slot // 2) * 4 + x * 2 + slot % 2
            pl.semaphore_signal(
                barrier, inc=1, device_id=(peer, lax.rem(chan + turn, n_chan)), device_id_type=MESH
            )
    steps = lax.broadcasted_iota(jnp.int32, (SUB, LANES), 0).astype(F32)

    def lanes(b):
        return pl.ds(pl.multiple_of(b * LANES, LANES), LANES)

    for load in loads[:3]:
        load.wait()

    def end_block(b, _):
        at = lanes(b)
        s = k_ref[:, at].astype(F32) * v_ref[:, at].astype(F32)
        sig[:, at] = s
        found = []
        for m in range(modes):
            rate = rate_ref[pl.ds(m, 1), at]
            jump = jnp.exp(-float(SUB) * rate)
            total = s[:SUB]
            for t in range(1, tiles):
                total = total * jump + s[t * SUB:(t + 1) * SUB]
            total = total * jnp.exp(-rate * (float(SUB - 1) - steps))
            found.append(jnp.sum(total, axis=0, keepdims=True))
        state = jnp.concatenate(found, axis=0)
        fade = jnp.exp(-float(tok) * rate_ref[:, at])
        for p in range(per_block):
            ends[b * per_block + p] = state[p * rows:(p + 1) * rows].astype(BF16)
            fades[b * per_block + p] = fade[p * rows:(p + 1) * rows]
        return 0

    lax.fori_loop(0, blocks, end_block, 0)

    pl.semaphore_wait(barrier, n - 1 + (n_chan - 1) * 2 * line)

    def exchange(source, target, send_sem, recv_sem):
        copies = []
        for hop in sorted(range(1, n), key=lambda h: abs(h - n // 2)):
            peer = lax.rem(me + hop, n)
            copy = pltpu.make_async_remote_copy(
                src_ref=source.at[peer], dst_ref=target.at[me],
                send_sem=send_sem.at[hop], recv_sem=recv_sem.at[me],
                device_id=(peer, chan), device_id_type=MESH,
            )
            copy.start()
            copies.append(copy)
        target[me] = source[me]
        return copies

    def arrivals(target, send_sem, recv_sem):
        for hop in range(1, n):
            peer = lax.rem(me + hop, n)
            pltpu.make_async_remote_copy(
                src_ref=target.at[peer], dst_ref=target.at[peer],
                send_sem=send_sem.at[hop], recv_sem=recv_sem.at[peer],
                device_id=(peer, chan), device_id_type=MESH,
            ).wait_recv()

    across = me + 2 - 4 * x
    w_copies = []
    w_rows = chans // 8

    def swap(first, last):
        for part in range(first, last):
            at = pl.ds(part * w_rows, w_rows)
            copy = pltpu.make_async_remote_copy(
                src_ref=w_hbm.at[at], dst_ref=w_other.at[at],
                send_sem=w_send.at[part], recv_sem=w_recv.at[part],
                device_id=(across, chan), device_id_type=MESH,
            )
            copy.start()
            w_copies.append(copy)

    end_copies = exchange(ends, ends_all, end_send, end_recv)
    swap(0, 1)

    loads[3].wait()
    amp_ref[...] = amp_ref[...] * jnp.sqrt(one_minus_exp(2.0 * rate_ref[...]))

    padded[:SUB] = jnp.zeros((SUB, LANES), F32)

    def local_block(b, _):
        at = lanes(b)
        response = [jnp.zeros((SUB, LANES), F32)] * tiles
        for m in range(modes):
            rate = rate_ref[pl.ds(m, 1), at]
            jump = jnp.exp(-float(SUB) * rate)
            term = amp_ref[pl.ds(m, 1), at] * jnp.exp(-rate * steps)
            for t in range(tiles):
                response[t] = response[t] + term
                if t < tiles - 1:
                    term = term * jump
        padded[SUB:] = jnp.concatenate(response, axis=0)
        skip = skip_ref[:, at]
        totals = [skip * sig[t * SUB:(t + 1) * SUB, at] for t in range(tiles)]
        for lag in range(SUB):
            moved = [padded[pl.ds(SUB - lag + t * SUB, SUB)] for t in range(tiles)]
            for first in range(tiles):
                value = sig[pl.ds(first * SUB + lag, 1), at]
                for t in range(first, tiles):
                    totals[t] = totals[t] + moved[t - first] * value
        for t in range(tiles):
            local[t * SUB:(t + 1) * SUB, at] = totals[t]
        return 0

    lax.fori_loop(0, blocks, local_block, 0)

    arrivals(ends_all, end_send, end_recv)
    fade = fades[me]
    state = jnp.zeros((rows, LANES), F32)
    for i in range(n):
        starts_all[i] = state.astype(BF16)
        if i < n - 1:
            state = state * fade + ends_all[i].astype(F32)
    start_copies = exchange(starts_all, starts, start_send, start_recv)
    swap(1, 8)
    loads[4].wait()
    arrivals(starts, start_send, start_recv)

    own_rows = pl.multiple_of((2 * z + c) * tok, tok)

    def gate_block(b, _):
        at = lanes(b)
        held = [starts[b * per_block + p].astype(F32) for p in range(per_block)]
        totals = [local[t * SUB:(t + 1) * SUB, at] for t in range(tiles)]
        for m in range(modes):
            rate = rate_ref[pl.ds(m, 1), at]
            jump = jnp.exp(-float(SUB) * rate)
            start = held[m // rows][m % rows:m % rows + 1]
            term = (amp_ref[pl.ds(m, 1), at] * start) * jnp.exp(-rate * (steps + 1.0))
            for t in range(tiles):
                totals[t] = totals[t] + term
                if t < tiles - 1:
                    term = term * jump
        gated = q_ref[:, at].astype(F32) * jnp.concatenate(totals, axis=0)
        gathered[pl.ds(own_rows, tok), at] = gated.astype(BF16)
        return 0


    half_cols = chans // 2
    sib = me + 1 - 2 * c
    has_right = z < line - 1
    has_left = z > 0
    sent = []

    def piece(half, slot):
        return gathered.at[
            pl.ds(pl.multiple_of(slot * tok, tok), tok), pl.ds(half * half_cols, half_cols)
        ]

    def send(half, slot, peer, cond):
        copy = pltpu.make_async_remote_copy(
            src_ref=piece(half, slot), dst_ref=piece(half, slot),
            send_sem=gather_send.at[len(sent)], recv_sem=gather_recv.at[half * 2 * line + slot],
            device_id=(peer, chan), device_id_type=MESH,
        )
        sent.append((cond, copy))
        pl.when(cond)(copy.start)

    def receive(half, slot):
        pltpu.make_async_remote_copy(
            src_ref=piece(half, slot), dst_ref=piece(half, slot),
            send_sem=gather_send.at[0], recv_sem=gather_recv.at[half * 2 * line + slot],
            device_id=(sib, chan), device_id_type=MESH,
        ).wait_recv()

    out_chan = me // per_chan

    def part_copy(other, zz, to_core):
        to = zz * 4 + x * 2 + to_core
        owner = across if other else me
        slot = 2 * zz + to_core
        place = chan * per_chan + lax.rem(owner, per_chan)
        source = partial.at[
            pl.ds(pl.multiple_of((other * 2 * line + slot) * tok, tok), tok)
        ]
        remote = pltpu.make_async_remote_copy(
            src_ref=source, dst_ref=landed.at[place],
            send_sem=part_send.at[other * 2 * line + slot], recv_sem=part_recv.at[place],
            device_id=(to, out_chan), device_id_type=MESH,
        )
        here = pltpu.make_async_copy(source, landed.at[place], part_recv.at[place])
        return to, remote, here

    def project(zz, other):
        at = pl.ds(pl.multiple_of(zz * 2 * tok, 2 * tok), 2 * tok)
        to_rows = pl.ds(pl.multiple_of((other * line + zz) * 2 * tok, 2 * tok), 2 * tok)
        weights = w_other if other else w_ref
        partial[to_rows] = jnp.dot(
            gathered[at], weights[...], preferred_element_type=F32
        ).astype(BF16)
        for to_core in range(2):
            to, remote, here = part_copy(other, zz, to_core)
            stays = jnp.logical_and(to == me, out_chan == chan)
            pl.when(stays)(here.start)
            pl.when(jnp.logical_not(stays))(remote.start)

    for half in range(2):
        lax.fori_loop(half * blocks // 2, (half + 1) * blocks // 2, gate_block, 0)
        send(half, 2 * z + c, me + 4, has_right)
        send(half, 2 * z + c, me - 4, has_left)
        send(half, 2 * z + c, sib, z >= 0)
    loads[5].wait()
    for half in range(2):
        receive(half, 2 * z + 1 - c)
    project(z, 0)

    def others(last):
        for copy in w_copies:
            copy.wait_recv()
        project(z, 1)
        for d in range(1, last):
            for sign in (-1, 1):
                zz = z + sign * d
                there = zz >= 0 if sign < 0 else zz < line

                @pl.when(there)
                def _():
                    project(zz, 1)

    for d in range(1, line):
        if d == line - 1:
            others(d)
        for half in range(2):
            for sign in (-1, 1):
                zz = z + sign * d
                there = zz >= 0 if sign < 0 else zz < line
                onward = has_right if sign < 0 else has_left
                slot = 2 * zz + c

                @pl.when(there)
                def _():
                    receive(half, slot)

                send(half, slot, me - 4 * sign, jnp.logical_and(there, onward))
                send(half, slot, sib, there)
        for sign in (-1, 1):
            zz = z + sign * d
            there = zz >= 0 if sign < 0 else zz < line

            @pl.when(there)
            def _():
                for half in range(2):
                    receive(half, 2 * zz + 1 - c)
                project(zz, 0)
                if d == line - 1:
                    project(zz, 1)
    if line == 1:
        others(1)

    for i in range(per_chan):
        total = None
        for j in range(n_chan):
            slot = j * per_chan + i
            pltpu.make_async_remote_copy(
                src_ref=landed.at[slot], dst_ref=landed.at[slot],
                send_sem=part_send.at[0], recv_sem=part_recv.at[slot],
                device_id=(sib, chan), device_id_type=MESH,
            ).wait_recv()
            part = landed[slot].astype(F32)
            total = part if total is None else total + part
        out_ref[:, i * width:(i + 1) * width] = total.astype(BF16)

    for copy in end_copies + start_copies + w_copies:
        copy.wait_send()
    for cond, copy in sent:
        pl.when(cond)(copy.wait_send)
    for other in range(2):
        for slot in range(2 * line):
            to, remote, _ = part_copy(other, slot // 2, slot % 2)
            stays = jnp.logical_and(to == me, out_chan == chan)
            pl.when(jnp.logical_not(stays))(remote.wait_send)


def solution(mesh):
    n, n_chan = mesh.shape["seq"], mesh.shape["chan"]
    assert n % 4 == 0 and n % (4 * n_chan) == 0

    def body(gate_input, key_input, value_input, decay_rate, residue, skip_gain, out_weight):
        tok, chans = gate_input.shape
        modes = decay_rate.shape[0]
        width = out_weight.shape[1]
        rows = modes * chans // (LANES * n)
        hbm = pl.BlockSpec(memory_space=pltpu.HBM)
        vmem = pl.BlockSpec(memory_space=pltpu.VMEM)
        dma = pltpu.SemaphoreType.DMA
        states = pltpu.VMEM((n, rows, LANES), BF16)
        return pl.pallas_call(
            functools.partial(kernel, n, n_chan),
            out_shape=jax.ShapeDtypeStruct((tok, width * (n // n_chan)), BF16),
            in_specs=[hbm] * 5 + [vmem, hbm],
            out_specs=vmem,
            scratch_shapes=[
                pltpu.VMEM((tok, chans), BF16),
                pltpu.VMEM((tok, chans), BF16),
                pltpu.VMEM((tok, chans), BF16),
                pltpu.VMEM((modes, chans), F32),
                pltpu.VMEM((modes, chans), F32),
                pltpu.VMEM((chans, width), BF16),
                pltpu.VMEM((chans, width), BF16),
                dma((6,)), dma((8,)), dma((8,)),
                pltpu.VMEM((tok, chans), F32),
                pltpu.VMEM((tok, chans), F32),
                pltpu.VMEM((tok + SUB, LANES), F32),
                pltpu.VMEM((n, rows, LANES), F32),
                states, states, states, states,
                pltpu.VMEM((n * tok // 2, chans), BF16),
                pltpu.VMEM((n * tok, width), BF16),
                pltpu.VMEM((n, tok, width), BF16),
                dma((n,)), dma((n,)), dma((n,)), dma((n,)),
                dma((2 * n,)), dma((n,)), dma((n,)), dma((n,)),
            ],
            compiler_params=pltpu.CompilerParams(
                collective_id=0, has_side_effects=True, vmem_limit_bytes=67043328
            ),
            cost_estimate=pl.CostEstimate(
                flops=2 * n * tok * chans * width, bytes_accessed=4 * tok * chans, transcendentals=0
            ),
        )(gate_input, key_input, value_input, decay_rate, residue,
          skip_gain.reshape(1, chans), out_weight)

    return jax.shard_map(
        body,
        mesh=mesh,
        in_specs=(
            P("seq", "chan"),
            P("seq", "chan"),
            P("seq", "chan"),
            P(None, "chan"),
            P(None, "chan"),
            P("chan"),
            P("chan", "seq"),
        ),
        out_specs=P("seq", "chan"),
        check_vma=False,
    )
```

profile of v0, /device:TPU:5, one launch (start us, length us, event | category | flops | bytes accessed | tf_op | source)
XLA Modules:
  0.0 47.3 jit_solution(931469507882042555)
XLA Ops:
  0.0 45.6 %shard_map.73 = bf16[64,2048]{1,0:T(8,128)(2,1)} custom-call(bf16[64,2048]{1,0:T(8,128)(2,1)} %q_hbm.1, bf16[64,2048]{1,0:T(8,128)(2,1)} %k_hbm.1, bf16[64,2048]{1,0:T(8,128)(2,1)} %v_hbm.1, f32[16,2048]{1,0:T(8,128)} %rate_hbm.1, f32[16,2048]{1,0:T(8,128)} %residue_hbm.1, f32[1,2048]{1,0:T(1,128)} %bitcast.1, bf16[2048,256]{1,0:T(8,128)(2,1)} %w_hbm.1), custom_call_target="tpu_custom_call" | custom-call | flops 1073741824 | bytes 524288 | tf_op jit(solution)/shard_map/pallas_call | solution.py:350
  45.6 1.7 %copy.9 = bf16[64,2048]{1,0:T(8,128)(2,1)} copy(bf16[64,2048]{1,0:T(8,128)(2,1)} %shard_map.73) | data formatting | bytes 524288
where the time goes:
time: 47.5 us; the launch traced here: 47.3 us
  Pallas kernels  45.6 us (96%)
  local copies, waits for them, and re-layouts  1.67 us (4%)
    pallas_call x1, Pallas kernels, body(): pl.pallas_call(functools.partial(kernel, n, n_chan), out_shape=jax.ShapeD...  45.6 us
    unnamed x1, local copies, waits for them, and re-layouts  1.67 us

commit v1 on v0

v1 whole, which is shorter than its diff:
```python
import functools

import jax
import jax.numpy as jnp
from jax import lax
from jax.experimental import pallas as pl
from jax.experimental.pallas import tpu as pltpu
from jax.sharding import PartitionSpec as P

MESH = pl.DeviceIdType.MESH
F32 = jnp.float32
BF16 = jnp.bfloat16
LANES = 128
SUB = 8
SLAB = 4
HALVES = 2
PIECES = 2


def one_minus_exp(y):
    series = jnp.ones_like(y)
    for order in range(10, 1, -1):
        series = 1.0 - y * (1.0 / order) * series
    return jnp.where(y < 0.4, y * series, 1.0 - jnp.exp(-y))


def column_parts(width):
    return 2 if width % (2 * LANES) == 0 else 1


def kernel(
    n, n_chan,
    q_hbm, k_hbm, v_hbm, rate_hbm, residue_hbm, skip_hbm, w_hbm, out_hbm,
    q_ref, k_ref, v_ref, rate_ref, amp_ref, skip_ref, w_ref, w_other, load_sem, w_send, w_recv,
    sig, local, padded, ends, ends_all, carry_in, carry_out, starts_all, starts,
    gathered, partial, arrived, summed, landed, out_ref,
    ready, end_send, end_recv, carry_send, carry_recv, start_send, start_recv,
    line_send, line_recv, sib_send, sib_recv, cross_send, cross_recv, part_send, part_recv,
):
    loads = [
        pltpu.make_async_copy(source, target, load_sem.at[i])
        for i, (source, target) in enumerate([
            (k_hbm, k_ref), (v_hbm, v_ref), (rate_hbm, rate_ref),
            (residue_hbm, amp_ref), (skip_hbm, skip_ref), (q_hbm, q_ref), (w_hbm, w_ref),
        ])
    ]
    for load in loads:
        load.start()
    tok, chans = q_ref.shape
    modes = rate_ref.shape[0]
    blocks = chans // LANES
    width = w_ref.shape[1]
    per_chan = n // n_chan
    line = n // SLAB
    tiles = tok // SUB
    quarter_blocks = blocks // SLAB
    quarter = quarter_blocks * modes
    half = tok // HALVES
    parts = column_parts(width)
    cols = width // parts
    direct = width % LANES == 0

    me = lax.axis_index("seq")
    chan = lax.axis_index("chan")
    z = me // SLAB
    x = (me // 2) % 2
    c = me % 2
    qd = me % SLAB
    sib = me + 1 - 2 * c
    across = me + 2 - 4 * x
    has_right = z < line - 1
    has_left = z > 0
    out_chan = me // per_chan
    owner_plane = chan == out_chan

    def mate(turn):
        return me - qd + lax.rem(qd + turn, SLAB)

    barrier = pltpu.get_barrier_semaphore()

    def hello(seq, ch):
        pl.semaphore_signal(barrier, inc=1, device_id=(seq, ch), device_id_type=MESH)

    for turn in range(1, SLAB):
        hello(mate(turn), chan)
    pl.when(has_right)(lambda: hello(me + SLAB, chan))
    pl.when(has_left)(lambda: hello(me - SLAB, chan))
    for turn in range(1, n_chan):
        hello(me, lax.rem(chan + turn, n_chan))
    greeters = SLAB - 1 + n_chan - 1 + has_right.astype(jnp.int32) + has_left.astype(jnp.int32)
    steps = lax.broadcasted_iota(jnp.int32, (SUB, LANES), 0).astype(F32)

    def lanes(b):
        return pl.ds(pl.multiple_of(b * LANES, LANES), LANES)

    for load in loads[:3]:
        load.wait()

    def end_block(b, _):
        at = lanes(b)
        s = k_ref[:, at].astype(F32) * v_ref[:, at].astype(F32)
        sig[:, at] = s
        found = []
        for m in range(modes):
            rate = rate_ref[pl.ds(m, 1), at]
            jump = jnp.exp(-float(SUB) * rate)
            total = s[:SUB]
            for t in range(1, tiles):
                total = total * jump + s[t * SUB:(t + 1) * SUB]
            total = total * jnp.exp(-rate * (float(SUB - 1) - steps))
            found.append(jnp.sum(total, axis=0, keepdims=True))
        ends[pl.ds(pl.multiple_of(b * modes, modes), modes)] = jnp.concatenate(found, axis=0).astype(BF16)
        return 0

    lax.fori_loop(0, blocks, end_block, 0)

    pl.semaphore_wait(barrier, greeters)

    def quarter_rows(p):
        return pl.ds(pl.multiple_of(p * quarter, quarter), quarter)

    def slab_copy(source, target, send_sem, recv_sem, turn):
        return pltpu.make_async_remote_copy(
            src_ref=source, dst_ref=target, send_sem=send_sem, recv_sem=recv_sem,
            device_id=(mate(turn), chan), device_id_type=MESH,
        )

    def slab_wait(ref, sem):
        return slab_copy(ref, ref, sem, sem, 1)

    for turn in (2, 3, 1):
        slab_copy(ends.at[quarter_rows(lax.rem(qd + turn, SLAB))], ends_all.at[qd], end_send, end_recv, turn).start()
    ends_all[qd] = ends[quarter_rows(qd)]

    def swap(part, first, rows):
        at = (pl.ds(first, rows), pl.ds(part * cols, cols))
        pltpu.make_async_remote_copy(
            src_ref=w_hbm.at[at], dst_ref=w_other.at[at],
            send_sem=w_send.at[part], recv_sem=w_recv.at[part],
            device_id=(across, chan), device_id_type=MESH,
        ).start()

    def swapped(part):
        at = (slice(None), pl.ds(part * cols, cols))
        return pltpu.make_async_remote_copy(
            src_ref=w_other.at[at], dst_ref=w_other.at[at],
            send_sem=w_send.at[part], recv_sem=w_recv.at[part],
            device_id=(across, chan), device_id_type=MESH,
        )

    block_rows = LANES // 4
    middle_rows = chans * 7 // 32

    loads[3].wait()
    loads[4].wait()
    amp_ref[...] = amp_ref[...] * jnp.sqrt(one_minus_exp(2.0 * rate_ref[...]))

    padded[:SUB] = jnp.zeros((SUB, LANES), F32)

    def local_block(b, _):
        swap(0, pl.multiple_of(b * block_rows, block_rows), block_rows)
        at = lanes(b)
        response = [jnp.zeros((SUB, LANES), F32)] * tiles
        for m in range(modes):
            rate = rate_ref[pl.ds(m, 1), at]
            jump = jnp.exp(-float(SUB) * rate)
            term = amp_ref[pl.ds(m, 1), at] * jnp.exp(-rate * steps)
            for t in range(tiles):
                response[t] = response[t] + term
                if t < tiles - 1:
                    term = term * jump
        padded[SUB:] = jnp.concatenate(response, axis=0)
        skip = skip_ref[:, at]
        totals = [skip * sig[t * SUB:(t + 1) * SUB, at] for t in range(tiles)]
        for lag in range(SUB):
            moved = [padded[pl.ds(SUB - lag + t * SUB, SUB)] for t in range(tiles)]
            for first in range(tiles):
                value = sig[pl.ds(first * SUB + lag, 1), at]
                for t in range(first, tiles):
                    totals[t] = totals[t] + moved[t - first] * value
        for t in range(tiles):
            local[t * SUB:(t + 1) * SUB, at] = totals[t]
        return 0

    lax.fori_loop(0, blocks, local_block, 0)

    def signal_left():
        pl.semaphore_signal(ready, inc=1, device_id=(me - SLAB, chan), device_id_type=MESH)

    pl.when(z < line - 2)(lambda: pl.semaphore_wait(ready, 1))
    pl.when(jnp.logical_and(has_left, has_right))(signal_left)

    fades = jnp.concatenate(
        [jnp.exp(-float(tok) * rate_ref[:, lanes(qd * quarter_blocks + j)]) for j in range(quarter_blocks)], axis=0
    )
    slab_wait(ends_all.at[pl.ds(0, SLAB - 1)], end_recv).wait_recv()
    found = [ends_all[p].astype(F32) for p in range(SLAB)]
    slab_total = found[0]
    for p in range(1, SLAB):
        slab_total = slab_total * fades + found[p]
    slab_fade = (fades * fades) * (fades * fades)

    def carry_copy(hop):
        return pltpu.make_async_remote_copy(
            src_ref=carry_out, dst_ref=carry_in.at[z], send_sem=carry_send.at[hop - 1], recv_sem=carry_recv.at[z],
            device_id=(me + hop * SLAB, chan), device_id_type=MESH,
        )

    @pl.when(has_right)
    def _():
        carry_out[...] = slab_total.astype(BF16)
        for hop in range(1, line):
            pl.when(z + hop < line)(carry_copy(hop).start)

    @pl.when(has_left)
    def _():
        swap(0, blocks * block_rows, middle_rows)

    def collect(i, carry):
        pltpu.make_async_remote_copy(
            src_ref=carry_in.at[i], dst_ref=carry_in.at[i], send_sem=carry_send.at[0], recv_sem=carry_recv.at[i],
            device_id=(sib, chan), device_id_type=MESH,
        ).wait_recv()
        return carry * slab_fade + carry_in[i].astype(F32)

    carry = lax.fori_loop(0, z, collect, jnp.zeros((quarter, LANES), F32))

    state = carry
    for p in range(SLAB):
        starts_all[p] = state.astype(BF16)
        if p < SLAB - 1:
            state = state * fades + found[p]
    for turn in (2, 3, 1):
        slab_copy(
            starts_all.at[lax.rem(qd + turn, SLAB)], starts.at[quarter_rows(qd)], start_send, start_recv, turn
        ).start()
    starts[quarter_rows(qd)] = starts_all[qd]

    @pl.when(jnp.logical_not(has_left))
    def _():
        swap(0, blocks * block_rows, middle_rows)

    swap(0, blocks * block_rows + middle_rows, chans - blocks * block_rows - middle_rows)
    for part in range(1, parts):
        swap(part, 0, chans)
    loads[5].wait()
    slab_wait(starts.at[pl.ds(0, (SLAB - 1) * quarter)], start_recv).wait_recv()

    half_tiles = tiles // HALVES
    own_rows = [pl.multiple_of(((z * HALVES + h) * 2 + c) * half, half) for h in range(HALVES)]

    def gate_half(h):
        def gate_block(b, _):
            at = lanes(b)
            held = starts[pl.ds(pl.multiple_of(b * modes, modes), modes)].astype(F32)
            totals = [
                local[(h * half_tiles + t) * SUB:(h * half_tiles + t + 1) * SUB, at] for t in range(half_tiles)
            ]
            for m in range(modes):
                rate = rate_ref[pl.ds(m, 1), at]
                jump = jnp.exp(-float(SUB) * rate)
                term = (amp_ref[pl.ds(m, 1), at] * held[m:m + 1]) * jnp.exp(-rate * (steps + float(1 + h * half)))
                for t in range(half_tiles):
                    totals[t] = totals[t] + term
                    if t < half_tiles - 1:
                        term = term * jump
            q = q_ref[h * half:(h + 1) * half, at].astype(F32)
            gathered[pl.ds(own_rows[h], half), at] = (q * jnp.concatenate(totals, axis=0)).astype(BF16)
            return 0

        lax.fori_loop(0, blocks, gate_block, 0)

    piece_rows = half // PIECES

    def line_copy(h, p, zz, peer):
        at = pl.ds(pl.multiple_of(((zz * HALVES + h) * 2 + c) * half + p * piece_rows, piece_rows), piece_rows)
        return pltpu.make_async_remote_copy(
            src_ref=gathered.at[at], dst_ref=gathered.at[at],
            send_sem=line_send, recv_sem=line_recv.at[(zz * HALVES + h) * PIECES + p],
            device_id=(peer, chan), device_id_type=MESH,
        )

    def sib_copy(h, zz, core):
        at = pl.ds(pl.multiple_of(((zz * HALVES + h) * 2 + core) * half, half), half)
        return pltpu.make_async_remote_copy(
            src_ref=gathered.at[at], dst_ref=gathered.at[at],
            send_sem=sib_send, recv_sem=sib_recv.at[zz * HALVES + h],
            device_id=(sib, chan), device_id_type=MESH,
        )

    for h in range(HALVES):
        gate_half(h)
        for p in range(PIECES):
            pl.when(has_right)(line_copy(h, p, z, me + SLAB).start)
            pl.when(has_left)(line_copy(h, p, z, me - SLAB).start)
        sib_copy(h, z, c).start()
    loads[6].wait()

    def source(g, sign):
        d = g // HALVES
        zz = z - d if sign < 0 else z + d
        there = jnp.logical_and(zz >= 0, zz < line)
        if sign > 0:
            there = jnp.logical_and(there, d > 0)
        return g % HALVES, zz, there

    def relay(g):
        for p in range(PIECES):
            for sign in (-1, 1):
                h, zz, there = source(g, sign)

                @pl.when(there)
                def _():
                    line_copy(h, p, zz, sib).wait_recv()
                    pl.when(has_right if sign < 0 else has_left)(line_copy(h, p, zz, me - SLAB * sign).start)
                    if p == PIECES - 1:
                        sib_copy(h, zz, c).start()

    def unit_at(h, zz, other, part):
        rows = pl.multiple_of((zz * HALVES + h) * 2 * half, 2 * half)
        at = pl.ds(part * cols, cols) if other else slice(None)
        return rows, at, (zz * HALVES + h) * (1 + parts) + (1 + part if other else 0)

    def cross_copy(h, zz, other, part, sender, target):
        rows, at, unit = unit_at(h, zz, other, part)
        rows = pl.ds(rows, 2 * half)
        return pltpu.make_async_remote_copy(
            src_ref=partial.at[other, rows, at], dst_ref=arrived.at[sender, other, rows, at],
            send_sem=cross_send, recv_sem=cross_recv.at[sender - (sender > target).astype(jnp.int32), unit],
            device_id=(me, target), device_id_type=MESH,
        )

    def compute(g, other, part):
        for sign in (-1, 1):
            h, zz, there = source(g, sign)

            @pl.when(there)
            def _():
                rows, at, _ = unit_at(h, zz, other, part)
                if not other:
                    sib_copy(h, zz, 1 - c).wait_recv()
                weights = w_other if other else w_ref
                partial[other, pl.ds(rows, 2 * half), at] = jnp.dot(
                    gathered[pl.ds(rows, 2 * half)], weights[:, at], preferred_element_type=F32
                ).astype(BF16)

                @pl.when(jnp.logical_not(owner_plane))
                def _():
                    cross_copy(h, zz, other, part, chan, out_chan).start()

    def finish(g, other, part):
        for sign in (-1, 1):
            h, zz, there = source(g, sign)

            @pl.when(jnp.logical_and(there, owner_plane))
            def _():
                rows, at, _ = unit_at(h, zz, other, part)
                total = partial[other, pl.ds(rows, 2 * half), at].astype(F32)
                for turn in range(1, n_chan):
                    sender = lax.rem(chan + turn, n_chan)
                    cross_copy(h, zz, other, part, sender, chan).wait_recv()
                    total = total + arrived[sender, other, pl.ds(rows, 2 * half), at].astype(F32)
                summed[other, pl.ds(rows, 2 * half), at] = total.astype(BF16)
                place = lax.rem(across if other else me, per_chan)
                for core in range(2):
                    to = zz * SLAB + x * 2 + core
                    src = summed.at[other, pl.ds(rows + core * half, half), at]
                    rows_to = pl.ds(pl.multiple_of(h * half, half), half)
                    if direct:
                        start = pl.multiple_of(place * width + part * cols, LANES)
                        dst = out_hbm.at[rows_to, pl.ds(start, cols if other else width)]
                    else:
                        dst = landed.at[place, rows_to, at]
                    remote = pltpu.make_async_remote_copy(
                        src_ref=src, dst_ref=dst, send_sem=part_send, recv_sem=part_recv,
                        device_id=(to, chan), device_id_type=MESH,
                    )
                    here = pltpu.make_async_copy(src, dst, part_recv)
                    pl.when(to == me)(here.start)
                    pl.when(to != me)(remote.start)

    def each(first, last, body):
        def run(g, _):
            body(g)
            return 0

        lax.fori_loop(first, last, run, 0)

    last = line * HALVES - 1
    split = min(2 * HALVES, last)

    def first_steps(g):
        pl.when(g >= HALVES)(lambda: relay(g))
        compute(g, 0, 0)
        pl.when(g >= 1)(lambda: finish(g - 1, 0, 0))

    each(0, split, first_steps)
    swapped(0).wait_recv()
    each(0, split, lambda g: compute(g, 1, 0))
    finish(split - 1, 0, 0)

    def later_steps(g):
        relay(g)
        compute(g, 0, 0)
        compute(g, 1, 0)

        @pl.when(g == split)
        def _():
            each(0, split, lambda e: finish(e, 1, 0))

        @pl.when(g > split)
        def _():
            finish(g - 1, 0, 0)
            finish(g - 1, 1, 0)

    each(split, last, later_steps)
    for part in range(1, parts):
        swapped(part).wait_recv()
    if parts > 1:
        each(0, last, lambda g: [compute(g, 1, part) for part in range(1, parts)])
    if last > split:
        finish(last - 1, 0, 0)
        finish(last - 1, 1, 0)
    else:
        each(0, split, lambda e: finish(e, 1, 0))
    if last >= HALVES:
        relay(last)
    compute(last, 0, 0)
    for part in range(parts):
        compute(last, 1, part)
    if parts > 1:
        each(0, last, lambda g: [finish(g, 1, part) for part in range(1, parts)])
    finish(last, 0, 0)
    for part in range(parts):
        finish(last, 1, part)

    def drained(ref, sem):
        return pltpu.make_async_remote_copy(
            src_ref=ref, dst_ref=ref, send_sem=sem, recv_sem=sem, device_id=(sib, chan), device_id_type=MESH,
        )

    if direct:
        drained(out_hbm, part_recv).wait_recv()
    else:
        drained(landed, part_recv).wait_recv()
        for i in range(per_chan):
            out_ref[:, i * width:(i + 1) * width] = landed[i]
        store = pltpu.make_async_copy(out_ref, out_hbm, load_sem.at[0])
        store.start()
        store.wait()

    drained(ends_all.at[pl.ds(0, SLAB - 1)], end_send).wait_send()
    drained(starts_all.at[pl.ds(0, SLAB - 1)], start_send).wait_send()
    for hop in range(1, line):
        pl.when(z + hop < line)(carry_copy(hop).wait_send)
    for part in range(parts):
        swapped(part).wait_send()
    inner = jnp.logical_and(has_left, has_right)
    if line > 2:
        pl.when(inner)(drained(gathered.at[pl.ds(0, (line + 1) * tok)], line_send).wait_send)
    if line > 1:
        pl.when(jnp.logical_not(inner))(drained(gathered.at[pl.ds(0, tok)], line_send).wait_send)
    drained(gathered.at[pl.ds(0, line * tok)], sib_send).wait_send()
    pl.when(owner_plane)(drained(summed.at[:, pl.ds(0, (2 * line - 1) * tok)], part_send).wait_send)
    pl.when(jnp.logical_not(owner_plane))(drained(partial, cross_send).wait_send)


def solution(mesh):
    n, n_chan = mesh.shape["seq"], mesh.shape["chan"]
    assert n % SLAB == 0 and n % (SLAB * n_chan) == 0

    def body(gate_input, key_input, value_input, decay_rate, residue, skip_gain, out_weight):
        tok, chans = gate_input.shape
        modes = decay_rate.shape[0]
        width = out_weight.shape[1]
        line = n // SLAB
        parts = column_parts(width)
        quarter = modes * chans // (LANES * SLAB)
        rows = 2 * line * tok
        units = line * HALVES * (1 + parts)
        direct = width % LANES == 0
        hbm = pl.BlockSpec(memory_space=pltpu.HBM)
        dma = pltpu.SemaphoreType.DMA
        slab_states = pltpu.VMEM((SLAB, quarter, LANES), BF16)
        all_states = pltpu.VMEM((SLAB * quarter, LANES), BF16)
        return pl.pallas_call(
            functools.partial(kernel, n, n_chan),
            out_shape=jax.ShapeDtypeStruct((tok, width * (n // n_chan)), BF16),
            in_specs=[hbm] * 7,
            out_specs=pl.BlockSpec(memory_space=pl.ANY),
            scratch_shapes=[
                pltpu.VMEM((tok, chans), BF16),
                pltpu.VMEM((tok, chans), BF16),
                pltpu.VMEM((tok, chans), BF16),
                pltpu.VMEM((modes, chans), F32),
                pltpu.VMEM((modes, chans), F32),
                pltpu.VMEM((1, chans), F32),
                pltpu.VMEM((chans, width), BF16),
                pltpu.VMEM((chans, width), BF16),
                dma((7,)), dma((parts,)), dma((parts,)),
                pltpu.VMEM((tok, chans), F32),
                pltpu.VMEM((tok, chans), F32),
                pltpu.VMEM((tok + SUB, LANES), F32),
                all_states, slab_states, pltpu.VMEM((line, quarter, LANES), BF16), pltpu.VMEM((quarter, LANES), BF16),
                slab_states, all_states,
                pltpu.VMEM((rows, chans), BF16),
                pltpu.VMEM((2, rows, width), BF16),
                pltpu.VMEM((n_chan, 2, rows, width), BF16),
                pltpu.VMEM((2, rows, width), BF16),
                pltpu.VMEM((1, 16, LANES) if direct else (n // n_chan, tok, width), BF16),
                pltpu.VMEM((16, LANES) if direct else (tok, width * (n // n_chan)), BF16),
                pltpu.SemaphoreType.REGULAR, dma(()), dma(()), dma((line,)), dma((line,)), dma(()), dma(()),
                dma(()), dma((line * HALVES * PIECES,)), dma(()), dma((line * HALVES,)),
                dma(()), dma((max(n_chan - 1, 1), units)), dma(()), dma(()),
            ],
            compiler_params=pltpu.CompilerParams(
                collective_id=0, has_side_effects=True, vmem_limit_bytes=40 * 2**20
            ),
            cost_estimate=pl.CostEstimate(
                flops=2 * n * tok * chans * width, bytes_accessed=4 * tok * chans, transcendentals=0
            ),
        )(*[
            pltpu.with_memory_space_constraint(array, pltpu.HBM)
            for array in (
                gate_input, key_input, value_input, decay_rate, residue, skip_gain.reshape(1, chans), out_weight
            )
        ])

    return jax.shard_map(
        body,
        mesh=mesh,
        in_specs=(
            P("seq", "chan"),
            P("seq", "chan"),
            P("seq", "chan"),
            P(None, "chan"),
            P(None, "chan"),
            P("chan"),
            P("chan", "seq"),
        ),
        out_specs=P("seq", "chan"),
        check_vma=False,
    )
```

time: 47.5 us -> 46.5 us (0.979)
  local copies, waits for them, and re-layouts: 1.67 us -> 0.71 us
    unnamed x1, local copies, waits for them, and re-layouts: 1.67 us -> 0.71 us
where the time goes in v1:
time: 46.5 us; the launch traced here: 46.3 us
  Pallas kernels  45.6 us (98%)
  local copies, waits for them, and re-layouts  0.71 us (2%)
    pallas_call x1, Pallas kernels, body(): pl.pallas_call(functools.partial(kernel, n, n_chan), out_shape=jax.ShapeD...  45.6 us

profile of v1, /device:TPU:5, one launch (start us, length us, event | category | flops | bytes accessed | tf_op | source)
XLA Modules:
  0.0 46.3 jit_solution(3494311023046996511)
XLA Ops:
  0.0 45.6 %shard_map.73 = bf16[64,2048]{1,0:T(8,128)(2,1)S(1)} custom-call(bf16[64,2048]{1,0:T(8,128)(2,1)} %q_hbm.1, bf16[64,2048]{1,0:T(8,128)(2,1)} %k_hbm.1, bf16[64,2048]{1,0:T(8,128)(2,1)} %v_hbm.1, f32[16,2048]{1,0:T(8,128)} %rate_hbm.1, f32[16,2048]{1,0:T(8,128)} %residue_hbm.1, f32[1,2048]{1,0:T(1,128)} %bitcast.1, bf16[2048,256]{1,0:T(8,128)(2,1)} %w_hbm.1), custom_call_target="tpu_custom_call" | custom-call | flops 1073741824 | bytes 524288 | tf_op jit(solution)/shard_map/pallas_call | solution.py:486
  45.6 0.7 %copy.9 = bf16[64,2048]{1,0:T(8,128)(2,1)} copy(bf16[64,2048]{1,0:T(8,128)(2,1)S(1)} %shard_map.73) | data formatting | bytes 524288

commit v2 on v1

v2 whole, which is shorter than its diff:
```python
import functools

import jax
import jax.numpy as jnp
from jax import lax
from jax.experimental import pallas as pl
from jax.experimental.pallas import tpu as pltpu
from jax.sharding import PartitionSpec as P

MESH = pl.DeviceIdType.MESH
F32 = jnp.float32
BF16 = jnp.bfloat16
LANES = 128
SUB = 8
SLAB = 4
HALVES = 2


def one_minus_exp(y):
    series = jnp.ones_like(y)
    for order in range(10, 1, -1):
        series = 1.0 - y * (1.0 / order) * series
    return jnp.where(y < 0.4, y * series, 1.0 - jnp.exp(-y))


def column_parts(width):
    return 2 if width % (2 * LANES) == 0 else 1


def kernel(
    n, n_chan,
    q_hbm, k_hbm, v_hbm, rate_hbm, residue_hbm, skip_hbm, w_hbm, out_hbm,
    q_ref, k_ref, v_ref, rate_ref, amp_ref, skip_ref, w_ref, w_other, load_sem, w_send, w_recv,
    sig, local, padded, ends, ends_all, carry_in, carry_out, starts_all, starts,
    local_out, q_near, local_near, starts_near, gathered, partial,
    ready, end_send, end_recv, carry_send, carry_recv, start_send, start_recv,
    near_send, near_recv, line_send, line_recv, sib_send, sib_recv, part_send, part_recv,
):
    loads = [
        pltpu.make_async_copy(source, target, load_sem.at[i])
        for i, (source, target) in enumerate([
            (k_hbm, k_ref), (v_hbm, v_ref), (rate_hbm, rate_ref),
            (residue_hbm, amp_ref), (skip_hbm, skip_ref), (q_hbm, q_ref), (w_hbm, w_ref),
        ])
    ]
    for load in loads:
        load.start()
    tok, chans = q_ref.shape
    modes = rate_ref.shape[0]
    blocks = chans // LANES
    width = w_ref.shape[1]
    per_chan = n // n_chan
    line = n // SLAB
    tiles = tok // SUB
    quarter_blocks = blocks // SLAB
    quarter = quarter_blocks * modes
    half = tok // HALVES
    parts = column_parts(width)
    cols = width // parts
    direct = width % LANES == 0

    me = lax.axis_index("seq")
    chan = lax.axis_index("chan")
    z = me // SLAB
    x = (me // 2) % 2
    c = me % 2
    qd = me % SLAB
    sib = me + 1 - 2 * c
    across = me + 2 - 4 * x
    has_right = z < line - 1
    has_left = z > 0
    out_chan = me // per_chan
    owner_plane = chan == out_chan
    giver = jnp.logical_or(z == 1, z == line - 2)
    taker = jnp.logical_not(jnp.logical_and(has_left, has_right))
    near = jnp.where(z == 0, 1, line - 2)
    taken_by = jnp.where(z == 1, me - SLAB, me + SLAB)

    def quarter_of(turn):
        return (x if turn < 2 else 1 - x) * 2 + (c if turn % 2 == 0 else 1 - c)

    def mate(turn):
        return me - qd + quarter_of(turn)

    barrier = pltpu.get_barrier_semaphore()

    def hello(seq, ch):
        pl.semaphore_signal(barrier, inc=1, device_id=(seq, ch), device_id_type=MESH)

    for turn in range(1, SLAB):
        hello(mate(turn), chan)
    pl.when(has_right)(lambda: hello(me + SLAB, chan))
    pl.when(has_left)(lambda: hello(me - SLAB, chan))
    for turn in range(1, n_chan):
        hello(me, lax.rem(chan + turn, n_chan))
    greeters = SLAB - 1 + n_chan - 1 + has_right.astype(jnp.int32) + has_left.astype(jnp.int32)
    steps = lax.broadcasted_iota(jnp.int32, (SUB, LANES), 0).astype(F32)

    def lanes(b):
        return pl.ds(pl.multiple_of(b * LANES, LANES), LANES)

    for load in loads[:3]:
        load.wait()

    def end_block(b, _):
        at = lanes(b)
        s = k_ref[:, at].astype(F32) * v_ref[:, at].astype(F32)
        sig[:, at] = s
        found = []
        for m in range(modes):
            rate = rate_ref[pl.ds(m, 1), at]
            jump = jnp.exp(-float(SUB) * rate)
            total = s[:SUB]
            for t in range(1, tiles):
                total = total * jump + s[t * SUB:(t + 1) * SUB]
            total = total * jnp.exp(-rate * (float(SUB - 1) - steps))
            found.append(jnp.sum(total, axis=0, keepdims=True))
        ends[pl.ds(pl.multiple_of(b * modes, modes), modes)] = jnp.concatenate(found, axis=0).astype(BF16)
        return 0

    lax.fori_loop(0, blocks, end_block, 0)

    pl.semaphore_wait(barrier, greeters)

    def quarter_rows(p):
        return pl.ds(pl.multiple_of(p * quarter, quarter), quarter)

    def slab_copy(source, target, send_sem, recv_sem, turn):
        return pltpu.make_async_remote_copy(
            src_ref=source, dst_ref=target, send_sem=send_sem, recv_sem=recv_sem,
            device_id=(mate(turn), chan), device_id_type=MESH,
        )

    def slab_wait(ref, sem):
        return slab_copy(ref, ref, sem, sem, 1)

    for turn in (2, 3, 1):
        slab_copy(ends.at[quarter_rows(quarter_of(turn))], ends_all.at[qd], end_send, end_recv, turn).start()
    ends_all[qd] = ends[quarter_rows(qd)]

    def near_copy(source, target, kind):
        return pltpu.make_async_remote_copy(
            src_ref=source, dst_ref=target, send_sem=near_send.at[kind], recv_sem=near_recv.at[kind],
            device_id=(taken_by, chan), device_id_type=MESH,
        )

    def give_q(first, rows):
        near_copy(q_hbm.at[pl.ds(first, rows)], q_near.at[pl.ds(first, rows)], 0).start()

    early_rows = tok * 3 // 4
    pl.when(giver)(lambda: give_q(0, early_rows))

    def swap(part, first, rows):
        at = (pl.ds(first, rows), pl.ds(part * cols, cols))
        pltpu.make_async_remote_copy(
            src_ref=w_hbm.at[at], dst_ref=w_other.at[at],
            send_sem=w_send.at[part], recv_sem=w_recv.at[part],
            device_id=(across, chan), device_id_type=MESH,
        ).start()

    def swapped(part):
        at = (slice(None), pl.ds(part * cols, cols))
        return pltpu.make_async_remote_copy(
            src_ref=w_other.at[at], dst_ref=w_other.at[at],
            send_sem=w_send.at[part], recv_sem=w_recv.at[part],
            device_id=(across, chan), device_id_type=MESH,
        )

    block_rows = LANES // 4
    middle_rows = chans * 7 // 32

    loads[3].wait()
    loads[4].wait()
    amp_ref[...] = amp_ref[...] * jnp.sqrt(one_minus_exp(2.0 * rate_ref[...]))

    padded[:SUB] = jnp.zeros((SUB, LANES), F32)

    def local_block(b, _):
        swap(0, pl.multiple_of(b * block_rows, block_rows), block_rows)
        at = lanes(b)
        response = [jnp.zeros((SUB, LANES), F32)] * tiles
        for m in range(modes):
            rate = rate_ref[pl.ds(m, 1), at]
            jump = jnp.exp(-float(SUB) * rate)
            term = amp_ref[pl.ds(m, 1), at] * jnp.exp(-rate * steps)
            for t in range(tiles):
                response[t] = response[t] + term
                if t < tiles - 1:
                    term = term * jump
        padded[SUB:] = jnp.concatenate(response, axis=0)
        skip = skip_ref[:, at]
        totals = [skip * sig[t * SUB:(t + 1) * SUB, at] for t in range(tiles)]
        for lag in range(SUB):
            moved = [padded[pl.ds(SUB - lag + t * SUB, SUB)] for t in range(tiles)]
            for first in range(tiles):
                value = sig[pl.ds(first * SUB + lag, 1), at]
                for t in range(first, tiles):
                    totals[t] = totals[t] + moved[t - first] * value
        totals = jnp.concatenate(totals, axis=0)
        local[:, at] = totals
        local_out[:, at] = totals.astype(BF16)
        return 0

    lax.fori_loop(0, blocks, local_block, 0)

    def signal_left():
        pl.semaphore_signal(ready, inc=1, device_id=(me - SLAB, chan), device_id_type=MESH)

    pl.when(z < line - 2)(lambda: pl.semaphore_wait(ready, 1))
    pl.when(jnp.logical_and(has_left, has_right))(signal_left)

    fades = jnp.concatenate(
        [jnp.exp(-float(tok) * rate_ref[:, lanes(qd * quarter_blocks + j)]) for j in range(quarter_blocks)], axis=0
    )
    slab_wait(ends_all.at[pl.ds(0, SLAB - 1)], end_recv).wait_recv()
    found = [ends_all[p].astype(F32) for p in range(SLAB)]
    slab_total = found[0]
    for p in range(1, SLAB):
        slab_total = slab_total * fades + found[p]
    slab_fade = (fades * fades) * (fades * fades)

    def carry_copy(hop):
        return pltpu.make_async_remote_copy(
            src_ref=carry_out, dst_ref=carry_in.at[z], send_sem=carry_send.at[hop - 1], recv_sem=carry_recv.at[z],
            device_id=(me + hop * SLAB, chan), device_id_type=MESH,
        )

    @pl.when(has_right)
    def _():
        carry_out[...] = slab_total.astype(BF16)
        for hop in range(1, line):
            pl.when(z + hop < line)(carry_copy(hop).start)

    @pl.when(giver)
    def _():
        give_q(early_rows, tok - early_rows)
        near_copy(local_out, local_near, 1).start()

    @pl.when(has_left)
    def _():
        swap(0, blocks * block_rows, middle_rows)

    def collect(i, carry):
        pltpu.make_async_remote_copy(
            src_ref=carry_in.at[i], dst_ref=carry_in.at[i], send_sem=carry_send.at[0], recv_sem=carry_recv.at[i],
            device_id=(sib, chan), device_id_type=MESH,
        ).wait_recv()
        return carry * slab_fade + carry_in[i].astype(F32)

    carry = lax.fori_loop(0, z, collect, jnp.zeros((quarter, LANES), F32))

    state = carry
    for p in range(SLAB):
        starts_all[p] = state.astype(BF16)
        if p < SLAB - 1:
            state = state * fades + found[p]
    for turn in (2, 3, 1):
        slab_copy(
            starts_all.at[quarter_of(turn)], starts.at[quarter_rows(qd)], start_send, start_recv.at[turn - 1], turn
        ).start()
    starts[quarter_rows(qd)] = starts_all[qd]

    @pl.when(jnp.logical_not(has_left))
    def _():
        swap(0, blocks * block_rows, middle_rows)

    swap(0, blocks * block_rows + middle_rows, chans - blocks * block_rows - middle_rows)
    for part in range(1, parts):
        swap(part, 0, chans)
    loads[5].wait()

    def gate(zz, q_from, local_from, starts_from, first, count):
        targets = [
            pl.ds(pl.multiple_of(((zz * HALVES + h) * 2 + c) * half, half), half) for h in range(HALVES)
        ]

        def gate_block(b, _):
            at = lanes(b)
            held = starts_from[pl.ds(pl.multiple_of(b * modes, modes), modes)].astype(F32)
            found = local_from[:, at].astype(F32)
            totals = [found[t * SUB:(t + 1) * SUB] for t in range(tiles)]
            for m in range(modes):
                rate = rate_ref[pl.ds(m, 1), at]
                jump = jnp.exp(-float(SUB) * rate)
                term = (amp_ref[pl.ds(m, 1), at] * held[m:m + 1]) * jnp.exp(-rate * (steps + 1.0))
                for t in range(tiles):
                    totals[t] = totals[t] + term
                    if t < tiles - 1:
                        term = term * jump
            gated = (q_from[:, at].astype(F32) * jnp.concatenate(totals, axis=0)).astype(BF16)
            for h in range(HALVES):
                gathered[targets[h], at] = gated[h * half:(h + 1) * half]
            return 0

        lax.fori_loop(first, first + count, gate_block, 0)

    quarter_cols = chans // SLAB

    def line_copy(h, turn, zz, peer):
        at = (
            pl.ds(pl.multiple_of(((zz * HALVES + h) * 2 + c) * half, half), half),
            pl.ds(pl.multiple_of(quarter_of(turn) * quarter_cols, quarter_cols), quarter_cols),
        )
        return pltpu.make_async_remote_copy(
            src_ref=gathered.at[at], dst_ref=gathered.at[at],
            send_sem=line_send, recv_sem=line_recv.at[(zz * HALVES + h) * SLAB + turn],
            device_id=(peer, chan), device_id_type=MESH,
        )

    def sib_copy(h, zz, core):
        at = pl.ds(pl.multiple_of(((zz * HALVES + h) * 2 + core) * half, half), half)
        return pltpu.make_async_remote_copy(
            src_ref=gathered.at[at], dst_ref=gathered.at[at],
            send_sem=sib_send, recv_sem=sib_recv.at[zz * HALVES + h],
            device_id=(sib, chan), device_id_type=MESH,
        )

    def send_own(pieces):
        for h, turn in pieces:
            pl.when(jnp.logical_and(has_right, z != line - 2))(line_copy(h, turn, z, me + SLAB).start)
            pl.when(jnp.logical_and(has_left, z != 1))(line_copy(h, turn, z, me - SLAB).start)

    order = [[(0, 0), (1, 0), (0, 1), (1, 1), (0, 2), (0, 3)], [(1, 2), (1, 3)]]
    for turn in range(SLAB):
        if turn:
            slab_wait(starts.at[quarter_rows(quarter_of(turn))], start_recv.at[turn - 1]).wait_recv()
        gate(z, q_ref, local, starts, quarter_of(turn) * quarter_blocks, quarter_blocks)
        if turn < 2:
            send_own(order[0][2 * turn:2 * turn + 2])
    pl.when(giver)(near_copy(starts, starts_near, 2).start)
    send_own(order[0][4:] + order[1])
    for h in range(HALVES):
        sib_copy(h, z, c).start()
    loads[6].wait()

    def source(d, sign):
        zz = z - d if sign < 0 else z + d
        there = jnp.logical_and(zz >= 0, zz < line)
        if sign > 0:
            there = jnp.logical_and(there, d > 0)
        return zz, there

    def relay(d, h):
        taking = jnp.logical_and(taker, d == 1)
        if h == 0:
            @pl.when(taking)
            def _():
                near_copy(q_near, q_near, 0).wait_recv()
                near_copy(local_near, local_near, 1).wait_recv()
                near_copy(starts_near, starts_near, 2).wait_recv()
                gate(near, q_near, local_near, starts_near, 0, blocks)
                for e in range(HALVES):
                    sib_copy(e, near, c).start()

        for e, turn in order[h]:
            for sign in (-1, 1):
                zz, there = source(d, sign)

                @pl.when(jnp.logical_and(there, jnp.logical_not(taking)))
                def _():
                    line_copy(e, turn, zz, sib).wait_recv()
                    pl.when(has_right if sign < 0 else has_left)(line_copy(e, turn, zz, me - SLAB * sign).start)
                    if (e, turn) == order[h][-1]:
                        sib_copy(h, zz, c).start()

    def compute(d, halves, other, part):
        for sign in (-1, 1):
            zz, there = source(d, sign)

            @pl.when(there)
            def _():
                if not other:
                    for h in halves:
                        sib_copy(h, zz, 1 - c).wait_recv()
                size = 2 * half * len(halves)
                rows = pl.ds(pl.multiple_of((zz * HALVES + halves[0]) * 2 * half, 2 * half), size)
                at = pl.ds(part * cols, cols) if other else slice(None)
                weights = w_other if other else w_ref
                partial[other, rows, at] = jnp.dot(
                    gathered[rows], weights[:, at], preferred_element_type=F32
                ).astype(BF16)
                place = lax.rem(across if other else me, per_chan)
                for h in halves:
                    for core in range(2):
                        to = zz * SLAB + x * 2 + core
                        sent = pl.ds(pl.multiple_of(((zz * HALVES + h) * 2 + core) * half, half), half)
                        src = partial.at[other, sent, at]
                        if direct:
                            start = pl.multiple_of(place * width + part * cols, LANES)
                            dst = out_hbm.at[chan, pl.ds(h * half, half), pl.ds(start, cols if other else width)]
                        else:
                            dst = out_hbm.at[chan, place, pl.ds(h * half, half), at]
                        remote = pltpu.make_async_remote_copy(
                            src_ref=src, dst_ref=dst, send_sem=part_send, recv_sem=part_recv,
                            device_id=(to, out_chan), device_id_type=MESH,
                        )
                        here = pltpu.make_async_copy(src, dst, part_recv)
                        stays = jnp.logical_and(to == me, owner_plane)
                        pl.when(stays)(here.start)
                        pl.when(jnp.logical_not(stays))(remote.start)

    def each(first, last, body):
        def run(g, _):
            body(g)
            return 0

        lax.fori_loop(first, last, run, 0)

    last = line - 1
    split = 2
    whole = tuple(range(HALVES))

    compute(0, whole, 0, 0)

    def relay_whole(d):
        for h in range(HALVES):
            relay(d, h)

    relay_whole(1)
    swapped(0).wait_recv()
    compute(0, whole, 1, 0)
    each(split, last, relay_whole)

    def later_steps(d):
        compute(d, whole, 0, 0)
        compute(d, whole, 1, 0)

    each(1, last, later_steps)
    for h in range(HALVES):
        relay(last, h)
    for part in range(1, parts):
        swapped(part).wait_recv()
        each(0, last, lambda d: compute(last - 1 - d, whole, 1, part))
    compute(last, whole, 0, 0)
    for part in range(parts):
        compute(last, whole, 1, part)

    def drained(ref, sem):
        return pltpu.make_async_remote_copy(
            src_ref=ref, dst_ref=ref, send_sem=sem, recv_sem=sem, device_id=(sib, chan), device_id_type=MESH,
        )

    drained(out_hbm, part_recv).wait_recv()

    drained(ends_all.at[pl.ds(0, SLAB - 1)], end_send).wait_send()
    drained(starts_all.at[pl.ds(0, SLAB - 1)], start_send).wait_send()
    for hop in range(1, line):
        pl.when(z + hop < line)(carry_copy(hop).wait_send)
    for part in range(parts):
        swapped(part).wait_send()
    inner = jnp.logical_not(jnp.logical_or(taker, giver))
    pl.when(inner)(drained(gathered.at[pl.ds(0, (line + 1) * tok)], line_send).wait_send)
    pl.when(taker)(drained(gathered.at[pl.ds(0, tok)], line_send).wait_send)
    pl.when(giver)(drained(gathered.at[pl.ds(0, line * tok)], line_send).wait_send)
    for kind, ref in enumerate((q_near, local_near, starts_near)):
        pl.when(giver)(near_copy(ref, ref, kind).wait_send)
    drained(gathered.at[pl.ds(0, line * tok)], sib_send).wait_send()
    pl.when(owner_plane)(drained(partial.at[:, pl.ds(0, (2 * line - 1) * tok)], part_send).wait_send)
    pl.when(jnp.logical_not(owner_plane))(drained(partial, part_send).wait_send)


def solution(mesh):
    n, n_chan = mesh.shape["seq"], mesh.shape["chan"]
    assert n % (SLAB * n_chan) == 0 and n >= 4 * SLAB

    def body(gate_input, key_input, value_input, decay_rate, residue, skip_gain, out_weight):
        tok, chans = gate_input.shape
        modes = decay_rate.shape[0]
        width = out_weight.shape[1]
        line = n // SLAB
        quarter = modes * chans // (LANES * SLAB)
        rows = 2 * line * tok
        direct = width % LANES == 0
        hbm = pl.BlockSpec(memory_space=pltpu.HBM)
        dma = pltpu.SemaphoreType.DMA
        slab_states = pltpu.VMEM((SLAB, quarter, LANES), BF16)
        all_states = pltpu.VMEM((SLAB * quarter, LANES), BF16)
        per_chan = n // n_chan
        landing = (n_chan, tok, width * per_chan) if direct else (n_chan, per_chan, tok, width)
        landed = pl.pallas_call(
            functools.partial(kernel, n, n_chan),
            out_shape=jax.ShapeDtypeStruct(landing, BF16),
            in_specs=[hbm] * 7,
            out_specs=pl.BlockSpec(memory_space=pl.ANY),
            scratch_shapes=[
                pltpu.VMEM((tok, chans), BF16),
                pltpu.VMEM((tok, chans), BF16),
                pltpu.VMEM((tok, chans), BF16),
                pltpu.VMEM((modes, chans), F32),
                pltpu.VMEM((modes, chans), F32),
                pltpu.VMEM((1, chans), F32),
                pltpu.VMEM((chans, width), BF16),
                pltpu.VMEM((chans, width), BF16),
                dma((7,)), dma((column_parts(width),)), dma((column_parts(width),)),
                pltpu.VMEM((tok, chans), F32),
                pltpu.VMEM((tok, chans), F32),
                pltpu.VMEM((tok + SUB, LANES), F32),
                all_states, slab_states, pltpu.VMEM((line, quarter, LANES), BF16), pltpu.VMEM((quarter, LANES), BF16),
                slab_states, all_states,
                pltpu.VMEM((tok, chans), BF16), pltpu.VMEM((tok, chans), BF16), pltpu.VMEM((tok, chans), BF16), all_states,
                pltpu.VMEM((rows, chans), BF16),
                pltpu.VMEM((2, rows, width), BF16),
                pltpu.SemaphoreType.REGULAR, dma(()), dma(()), dma((line,)), dma((line,)), dma(()), dma((SLAB - 1,)),
                dma((3,)), dma((3,)), dma(()), dma((line * HALVES * SLAB,)), dma(()), dma((line * HALVES,)),
                dma(()), dma(()),
            ],
            compiler_params=pltpu.CompilerParams(
                collective_id=0, has_side_effects=True, vmem_limit_bytes=40 * 2**20
            ),
            cost_estimate=pl.CostEstimate(
                flops=2 * n * tok * chans * width, bytes_accessed=4 * tok * chans, transcendentals=0
            ),
        )(*[
            pltpu.with_memory_space_constraint(array, pltpu.HBM)
            for array in (
                gate_input, key_input, value_input, decay_rate, residue, skip_gain.reshape(1, chans), out_weight
            )
        ])
        mixed = landed[0].astype(F32)
        for j in range(1, n_chan):
            mixed = mixed + landed[j].astype(F32)
        mixed = mixed.astype(BF16)
        return mixed if direct else mixed.transpose(1, 0, 2).reshape(tok, width * per_chan)

    return jax.shard_map(
        body,
        mesh=mesh,
        in_specs=(
            P("seq", "chan"),
            P("seq", "chan"),
            P("seq", "chan"),
            P(None, "chan"),
            P(None, "chan"),
            P("chan"),
            P("chan", "seq"),
        ),
        out_specs=P("seq", "chan"),
        check_vma=False,
    )
```

time: 46.5 us -> 40.9 us (0.88)
  the two profiles are of different devices: /device:TPU:5 before, /device:TPU:17 now
where the time goes in v2:
time: 40.9 us; the launch traced here: 40.7 us
  Pallas kernels  39.9 us (98%)
  other arithmetic  0.77 us (2%)
    pallas_call x1, Pallas kernels, body(): pl.pallas_call(functools.partial(kernel, n, n_chan), out_shape=jax.ShapeD...  39.9 us

profile of v2, /device:TPU:17, one launch (start us, length us, event | category | flops | bytes accessed | tf_op | source)
XLA Modules:
  0.0 40.7 jit_solution(4381860906087058210)
XLA Ops:
  0.0 39.9 %shard_map.73 = bf16[2,64,2048]{2,1,0:T(8,128)(2,1)S(1)} custom-call(bf16[64,2048]{1,0:T(8,128)(2,1)} %q_hbm.1, bf16[64,2048]{1,0:T(8,128)(2,1)} %k_hbm.1, bf16[64,2048]{1,0:T(8,128)(2,1)} %v_hbm.1, f32[16,2048]{1,0:T(8,128)} %rate_hbm.1, f32[16,2048]{1,0:T(8,128)} %residue_hbm.1, f32[1,2048]{1,0:T(1,128)} %bitcast.3, bf16[2048,256]{1,0:T(8,128)(2,1)} %w_hbm.1), custom_call_target="tpu_custom_call" | custom-call | flops 1073741824 | bytes 524288 | tf_op jit(solution)/shard_map/pallas_call | solution.py:480
  39.9 0.8 %fusion = bf16[64,2048]{1,0:T(8,128)(2,1)} fusion(bf16[2,64,2048]{2,1,0:T(8,128)(2,1)S(1)} %shard_map.73), kind=kLoop, calls=%fused_computation.1 | loop fusion | flops 524288 | bytes 786432 | tf_op jit(solution)/shard_map/convert_element_type | solution.py:522

commit v3 on v2

--- a/solution.py
+++ b/solution.py
@@ -144,11 +144,14 @@
             device_id=(taken_by, chan), device_id_type=MESH,
         )
 
-    def give_q(first, rows):
-        near_copy(q_hbm.at[pl.ds(first, rows)], q_near.at[pl.ds(first, rows)], 0).start()
-
-    early_rows = tok * 3 // 4
-    pl.when(giver)(lambda: give_q(0, early_rows))
+    late_cols = pl.ds(pl.multiple_of((1 - x) * (chans // 2), chans // 2), chans // 2)
+    late_states = pl.ds(pl.multiple_of((1 - x) * 2 * quarter, 2 * quarter), 2 * quarter)
+    near_copies = [
+        near_copy(q_hbm.at[:, late_cols], q_near.at[:, late_cols], 0),
+        near_copy(local_out.at[:, late_cols], local_near.at[:, late_cols], 1),
+        near_copy(starts.at[late_states], starts_near.at[late_states], 2),
+    ]
+    pl.when(giver)(near_copies[0].start)
 
     def swap(part, first, rows):
         at = (pl.ds(first, rows), pl.ds(part * cols, cols))
@@ -231,10 +234,7 @@
         for hop in range(1, line):
             pl.when(z + hop < line)(carry_copy(hop).start)
 
-    @pl.when(giver)
-    def _():
-        give_q(early_rows, tok - early_rows)
-        near_copy(local_out, local_near, 1).start()
+    pl.when(giver)(near_copies[1].start)
 
     @pl.when(has_left)
     def _():
@@ -317,8 +317,11 @@
 
     def send_own(pieces):
         for h, turn in pieces:
-            pl.when(jnp.logical_and(has_right, z != line - 2))(line_copy(h, turn, z, me + SLAB).start)
-            pl.when(jnp.logical_and(has_left, z != 1))(line_copy(h, turn, z, me - SLAB).start)
+            right, left = has_right, has_left
+            if turn >= 2:
+                right, left = jnp.logical_and(right, z != line - 2), jnp.logical_and(left, z != 1)
+            pl.when(right)(line_copy(h, turn, z, me + SLAB).start)
+            pl.when(left)(line_copy(h, turn, z, me - SLAB).start)
 
     order = [[(0, 0), (1, 0), (0, 1), (1, 1), (0, 2), (0, 3)], [(1, 2), (1, 3)]]
     for turn in range(SLAB):
@@ -327,7 +330,7 @@
         gate(z, q_ref, local, starts, quarter_of(turn) * quarter_blocks, quarter_blocks)
         if turn < 2:
             send_own(order[0][2 * turn:2 * turn + 2])
-    pl.when(giver)(near_copy(starts, starts_near, 2).start)
+    pl.when(giver)(near_copies[2].start)
     send_own(order[0][4:] + order[1])
     for h in range(HALVES):
         sib_copy(h, z, c).start()
@@ -342,30 +345,36 @@
 
     def relay(d, h):
         taking = jnp.logical_and(taker, d == 1)
-        if h == 0:
-            @pl.when(taking)
-            def _():
-                near_copy(q_near, q_near, 0).wait_recv()
-                near_copy(local_near, local_near, 1).wait_recv()
-                near_copy(starts_near, starts_near, 2).wait_recv()
-                gate(near, q_near, local_near, starts_near, 0, blocks)
-                for e in range(HALVES):
-                    sib_copy(e, near, c).start()
-
         for e, turn in order[h]:
             for sign in (-1, 1):
                 zz, there = source(d, sign)
-
-                @pl.when(jnp.logical_and(there, jnp.logical_not(taking)))
+                if turn >= 2:
+                    there = jnp.logical_and(there, jnp.logical_not(taking))
+
+                @pl.when(there)
                 def _():
                     line_copy(e, turn, zz, sib).wait_recv()
                     pl.when(has_right if sign < 0 else has_left)(line_copy(e, turn, zz, me - SLAB * sign).start)
                     if (e, turn) == order[h][-1]:
                         sib_copy(h, zz, c).start()
 
-    def compute(d, halves, other, part):
+        if h == HALVES - 1:
+            @pl.when(taking)
+            def _():
+                for copy in near_copies:
+                    copy.wait_recv()
+                gate(near, q_near, local_near, starts_near, (1 - x) * (blocks // 2), blocks // 2)
+                for e in range(HALVES):
+                    sib_copy(e, near, c).start()
+
+    def relayless(sign):
+        return z == 0 if sign > 0 else z + 2 >= line
+
+    def compute(d, halves, other, part, side=None):
         for sign in (-1, 1):
             zz, there = source(d, sign)
+            if side is not None:
+                there = jnp.logical_and(there, relayless(sign) == side)
 
             @pl.when(there)
             def _():
@@ -410,22 +419,20 @@
     split = 2
     whole = tuple(range(HALVES))
 
+
+    for h in range(HALVES):
+        relay(1, h)
     compute(0, whole, 0, 0)
-
-    def relay_whole(d):
-        for h in range(HALVES):
-            relay(d, h)
-
-    relay_whole(1)
+    compute(1, whole, 0, 0, True)
+    each(split, last, lambda d: relay(d, 0))
     swapped(0).wait_recv()
+    compute(1, whole, 1, 0, True)
     compute(0, whole, 1, 0)
-    each(split, last, relay_whole)
-
-    def later_steps(d):
-        compute(d, whole, 0, 0)
-        compute(d, whole, 1, 0)
-
-    each(1, last, later_steps)
+    each(split, last, lambda d: relay(d, 1))
+    compute(1, whole, 0, 0, False)
+    each(split, last, lambda d: compute(d, whole, 0, 0))
+    compute(1, whole, 1, 0, False)
+    each(split, last, lambda d: compute(d, whole, 1, 0))
     for h in range(HALVES):
         relay(last, h)
     for part in range(1, parts):
@@ -451,9 +458,9 @@
     inner = jnp.logical_not(jnp.logical_or(taker, giver))
     pl.when(inner)(drained(gathered.at[pl.ds(0, (line + 1) * tok)], line_send).wait_send)
     pl.when(taker)(drained(gathered.at[pl.ds(0, tok)], line_send).wait_send)
-    pl.when(giver)(drained(gathered.at[pl.ds(0, line * tok)], line_send).wait_send)
-    for kind, ref in enumerate((q_near, local_near, starts_near)):
-        pl.when(giver)(near_copy(ref, ref, kind).wait_send)
+    pl.when(giver)(drained(gathered.at[pl.ds(0, line * tok + tok // 2)], line_send).wait_send)
+    for copy in near_copies:
+        pl.when(giver)(copy.wait_send)
     drained(gathered.at[pl.ds(0, line * tok)], sib_send).wait_send()
     pl.when(owner_plane)(drained(partial.at[:, pl.ds(0, (2 * line - 1) * tok)], part_send).wait_send)
     pl.when(jnp.logical_not(owner_plane))(drained(partial, part_send).wait_send)

time: 40.9 us -> 40 us (0.978)
  the two profiles are of different devices: /device:TPU:17 before, /device:TPU:5 now
where the time goes in v3:
time: 40 us; the launch traced here: 39.5 us
  Pallas kernels  38.7 us (97%)
  other arithmetic  0.77 us (2%)
    pallas_call x1, Pallas kernels, body(): pl.pallas_call(functools.partial(kernel, n, n_chan), out_shape=jax.ShapeD...  38.7 us

profile of v3, /device:TPU:5, one launch (start us, length us, event | category | flops | bytes accessed | tf_op | source)
XLA Modules:
  0.0 39.5 jit_solution(10579344019652763470)
XLA Ops:
  0.0 38.7 %shard_map.73 = bf16[2,64,2048]{2,1,0:T(8,128)(2,1)S(1)} custom-call(bf16[64,2048]{1,0:T(8,128)(2,1)} %q_hbm.1, bf16[64,2048]{1,0:T(8,128)(2,1)} %k_hbm.1, bf16[64,2048]{1,0:T(8,128)(2,1)} %v_hbm.1, f32[16,2048]{1,0:T(8,128)} %rate_hbm.1, f32[16,2048]{1,0:T(8,128)} %residue_hbm.1, f32[1,2048]{1,0:T(1,128)} %bitcast.3, bf16[2048,256]{1,0:T(8,128)(2,1)} %w_hbm.1), custom_call_target="tpu_custom_call" | custom-call | flops 1073741824 | bytes 524288 | tf_op jit(solution)/shard_map/pallas_call | solution.py:487
  38.7 0.8 %fusion = bf16[64,2048]{1,0:T(8,128)(2,1)} fusion(bf16[2,64,2048]{2,1,0:T(8,128)(2,1)S(1)} %shard_map.73), kind=kLoop, calls=%fused_computation.1 | loop fusion | flops 524288 | bytes 786432 | tf_op jit(solution)/shard_map/convert_element_type | solution.py:529

commit v4 on v3

--- a/solution.py
+++ b/solution.py
@@ -36,16 +36,22 @@
     ready, end_send, end_recv, carry_send, carry_recv, start_send, start_recv,
     near_send, near_recv, line_send, line_recv, sib_send, sib_recv, part_send, part_recv,
 ):
-    loads = [
-        pltpu.make_async_copy(source, target, load_sem.at[i])
+    tok, chans = q_ref.shape
+    first_loads = [
+        [
+            pltpu.make_async_copy(source.at[:, at], target.at[:, at], load_sem.at[7 + 3 * i + j])
+            for j, (source, target) in enumerate([(k_hbm, k_ref), (v_hbm, v_ref), (rate_hbm, rate_ref)])
+        ]
+        for i, at in enumerate([pl.ds(0, chans // 2), pl.ds(chans // 2, chans // 2)])
+    ]
+    loads = [None] * 3 + [
+        pltpu.make_async_copy(source, target, load_sem.at[3 + i])
         for i, (source, target) in enumerate([
-            (k_hbm, k_ref), (v_hbm, v_ref), (rate_hbm, rate_ref),
             (residue_hbm, amp_ref), (skip_hbm, skip_ref), (q_hbm, q_ref), (w_hbm, w_ref),
         ])
     ]
-    for load in loads:
+    for load in first_loads[0] + first_loads[1] + loads[3:]:
         load.start()
-    tok, chans = q_ref.shape
     modes = rate_ref.shape[0]
     blocks = chans // LANES
     width = w_ref.shape[1]
@@ -99,9 +105,6 @@
     def lanes(b):
         return pl.ds(pl.multiple_of(b * LANES, LANES), LANES)
 
-    for load in loads[:3]:
-        load.wait()
-
     def end_block(b, _):
         at = lanes(b)
         s = k_ref[:, at].astype(F32) * v_ref[:, at].astype(F32)
@@ -118,7 +121,10 @@
         ends[pl.ds(pl.multiple_of(b * modes, modes), modes)] = jnp.concatenate(found, axis=0).astype(BF16)
         return 0
 
-    lax.fori_loop(0, blocks, end_block, 0)
+    for i in range(2):
+        for load in first_loads[i]:
+            load.wait()
+        lax.fori_loop(i * blocks // 2, (i + 1) * blocks // 2, end_block, 0)
 
     pl.semaphore_wait(barrier, greeters)
 
@@ -437,8 +443,9 @@
         relay(last, h)
     for part in range(1, parts):
         swapped(part).wait_recv()
-        each(0, last, lambda d: compute(last - 1 - d, whole, 1, part))
-    compute(last, whole, 0, 0)
+        each(0, last, lambda d: compute(d, whole, 1, part))
+    for h in range(HALVES):
+        compute(last, (h,), 0, 0)
     for part in range(parts):
         compute(last, whole, 1, part)
 
@@ -498,7 +505,7 @@
                 pltpu.VMEM((1, chans), F32),
                 pltpu.VMEM((chans, width), BF16),
                 pltpu.VMEM((chans, width), BF16),
-                dma((7,)), dma((column_parts(width),)), dma((column_parts(width),)),
+                dma((13,)), dma((column_parts(width),)), dma((column_parts(width),)),
                 pltpu.VMEM((tok, chans), F32),
                 pltpu.VMEM((tok, chans), F32),
                 pltpu.VMEM((tok + SUB, LANES), F32),

time: 40 us -> 39.8 us (level)
  no operation moved by 1% of the time
where the time goes in v4:
time: 39.8 us; the launch traced here: 39.4 us
  Pallas kernels  38.7 us (97%)
  other arithmetic  0.77 us (2%)
    pallas_call x1, Pallas kernels, body(): pl.pallas_call(functools.partial(kernel, n, n_chan), out_shape=jax.ShapeD...  38.7 us

profile of v4, /device:TPU:5, one launch (start us, length us, event | category | flops | bytes accessed | tf_op | source)
XLA Modules:
  0.0 39.4 jit_solution(5712708052050416928)
XLA Ops:
  0.0 38.7 %shard_map.73 = bf16[2,64,2048]{2,1,0:T(8,128)(2,1)S(1)} custom-call(bf16[64,2048]{1,0:T(8,128)(2,1)} %q_hbm.1, bf16[64,2048]{1,0:T(8,128)(2,1)} %k_hbm.1, bf16[64,2048]{1,0:T(8,128)(2,1)} %v_hbm.1, f32[16,2048]{1,0:T(8,128)} %rate_hbm.1, f32[16,2048]{1,0:T(8,128)} %residue_hbm.1, f32[1,2048]{1,0:T(1,128)} %bitcast.3, bf16[2048,256]{1,0:T(8,128)(2,1)} %w_hbm.1), custom_call_target="tpu_custom_call" | custom-call | flops 1073741824 | bytes 524288 | tf_op jit(solution)/shard_map/pallas_call | solution.py:494
  38.7 0.8 %fusion = bf16[64,2048]{1,0:T(8,128)(2,1)} fusion(bf16[2,64,2048]{2,1,0:T(8,128)(2,1)S(1)} %shard_map.73), kind=kLoop, calls=%fused_computation.1 | loop fusion | flops 524288 | bytes 786432 | tf_op jit(solution)/shard_map/convert_element_type | solution.py:536

commit v5 on v4

--- a/solution.py
+++ b/solution.py
@@ -329,15 +329,15 @@
             pl.when(right)(line_copy(h, turn, z, me + SLAB).start)
             pl.when(left)(line_copy(h, turn, z, me - SLAB).start)
 
-    order = [[(0, 0), (1, 0), (0, 1), (1, 1), (0, 2), (0, 3)], [(1, 2), (1, 3)]]
+    order = [[(0, 0), (1, 0), (0, 1), (1, 1), (0, 2), (1, 2), (0, 3)], [(1, 3)]]
     for turn in range(SLAB):
         if turn:
             slab_wait(starts.at[quarter_rows(quarter_of(turn))], start_recv.at[turn - 1]).wait_recv()
         gate(z, q_ref, local, starts, quarter_of(turn) * quarter_blocks, quarter_blocks)
-        if turn < 2:
+        if turn < SLAB - 1:
             send_own(order[0][2 * turn:2 * turn + 2])
     pl.when(giver)(near_copies[2].start)
-    send_own(order[0][4:] + order[1])
+    send_own(order[0][6:] + order[1])
     for h in range(HALVES):
         sib_copy(h, z, c).start()
     loads[6].wait()

time: 39.8 us -> 39.6 us (level)
  Pallas kernels: 38.7 us -> 38.2 us
    pallas_call x1, Pallas kernels: 38.7 us -> 38.2 us  [body(): pl.pallas_call(functools.partial(kernel, n, n_chan), out_shape=jax.ShapeD...]
where the time goes in v5:
time: 39.6 us; the launch traced here: 39 us
  Pallas kernels  38.2 us (96%)
  other arithmetic  0.77 us (2%)
    pallas_call x1, Pallas kernels, body(): pl.pallas_call(functools.partial(kernel, n, n_chan), out_shape=jax.ShapeD...  38.2 us

profile of v5, /device:TPU:5, one launch (start us, length us, event | category | flops | bytes accessed | tf_op | source)
XLA Modules:
  0.0 39.0 jit_solution(5419347781195922948)
XLA Ops:
  0.0 38.2 %shard_map.73 = bf16[2,64,2048]{2,1,0:T(8,128)(2,1)S(1)} custom-call(bf16[64,2048]{1,0:T(8,128)(2,1)} %q_hbm.1, bf16[64,2048]{1,0:T(8,128)(2,1)} %k_hbm.1, bf16[64,2048]{1,0:T(8,128)(2,1)} %v_hbm.1, f32[16,2048]{1,0:T(8,128)} %rate_hbm.1, f32[16,2048]{1,0:T(8,128)} %residue_hbm.1, f32[1,2048]{1,0:T(1,128)} %bitcast.3, bf16[2048,256]{1,0:T(8,128)(2,1)} %w_hbm.1), custom_call_target="tpu_custom_call" | custom-call | flops 1073741824 | bytes 524288 | tf_op jit(solution)/shard_map/pallas_call | solution.py:494
  38.2 0.8 %fusion = bf16[64,2048]{1,0:T(8,128)(2,1)} fusion(bf16[2,64,2048]{2,1,0:T(8,128)(2,1)S(1)} %shard_map.73), kind=kLoop, calls=%fused_computation.1 | loop fusion | flops 524288 | bytes 786432 | tf_op jit(solution)/shard_map/convert_element_type | solution.py:536
